TPU v7x, 32 devices: a whole 2x2x4 slice. The times are simulated.
32 devices in a mesh: hb: 4 (over y, core), row: 2 (over x), col: 4 (over z).
Axes of the slice: x: 2, y: 2, z: 4, core: 2. Of those that a mesh axis runs over, the one named last changes fastest.
Arguments:
- cell_state: float32 [256, 8, 256, 512], P('hb', None, 'row', 'col'), may hold values from -6 to 6
- normalizer: float32 [256, 8, 256], P('hb', None, 'row'), may hold values from 0.1 to 4
- stabilizer: float32 [256, 8, 16], P('hb', None, 'row'), may hold values from -5 to 120
- queries: float32 [256, 8, 256], P('hb', None, 'row'), may hold values from 0.0125 to 0.1125
- key_vectors: float32 [256, 8, 256], P('hb', None, 'row'), may hold values from -6 to 6
- token_value_vectors: float32 [256, 8, 512], P('hb', None, 'col'), may hold values from -6 to 6
- input_gate: float32 [256, 8], P('hb'), may hold values from -3 to 3
- forget_gate: float32 [256, 8], P('hb'), may hold values from -1 to 5
- output_gate_logits: float32 [256, 8, 512], P('hb', None, 'col'), may hold values from -6 to 6
- norm_gain: float32 [8, 512], P(None, 'col'), may hold values from 0.5 to 1.5
- out_weight: bfloat16 [8, 512, 4096], P('hb', 'col', 'row'), may hold values from -0.09375 to 0.09375
Outputs:
- layer_out: float32 [256, 4096], P('hb', 'row')
- readout: float32 [256, 8, 512], P('hb', None, 'col')
- refreshed_cell: float32 [256, 8, 256, 512], P('hb', None, 'row', 'col')
- new_normal: float32 [256, 8, 256], P('hb', None, 'row')
- new_stab: float32 [256, 8, 16], P('hb', None, 'row')
All inputs are finite; a program needn't handle non-finite values.
Results may differ from a plain program's by a relative error of at most 0.0029.
Values may be sent and summed in bfloat16 or wider, within the bound.
A program may use at most 128 MiB of HBM per device.

v0:
```python
import jax
import jax.numpy as jnp
from jax import lax
from jax.sharding import PartitionSpec as P

DK = 256
DV = 512
RBLK = 16


def combined_all(part, axis, combine):
    gathered = jax.tree.map(lambda a: lax.all_gather(a, axis), part)

    def take(source):
        return jax.tree.map(lambda a: lax.dynamic_index_in_dim(a, source, 0, False), gathered)

    return lax.fori_loop(
        1, lax.axis_size(axis), lambda source, state: combine(state, take(source)), take(0)
    )


def combine_pairs(left_pair, right_pair):
    joined = jnp.maximum(left_pair[0], right_pair[0])
    left_scale = jnp.exp(left_pair[0] - joined)
    right_scale = jnp.exp(right_pair[0] - joined)
    numerator = left_pair[1] * left_scale[:, :, None] + right_pair[1] * right_scale[:, :, None]
    denom = left_pair[2] * left_scale + right_pair[2] * right_scale
    return (joined, numerator, denom)


def local(
    cell_state,
    normalizer,
    stabilizer,
    queries,
    key_vectors,
    token_value_vectors,
    input_gate,
    forget_gate,
    output_gate_logits,
    norm_gain,
    out_weight,
):
    carried = jax.nn.log_sigmoid(forget_gate)[:, :, None] + stabilizer
    fresh = jnp.maximum(carried, input_gate[:, :, None])
    keep = jnp.repeat(jnp.exp(carried - fresh), RBLK, axis=2)
    admit = jnp.repeat(jnp.exp(input_gate[:, :, None] - fresh), RBLK, axis=2)
    scaled = key_vectors * DK ** (-0.5)
    refreshed_cell = (
        keep[:, :, :, None] * cell_state
        + (admit * scaled)[:, :, :, None] * token_value_vectors[:, :, None, :]
    )
    new_normal = keep * normalizer + admit * scaled
    local_top = jnp.max(fresh, axis=2)
    weight_matrix = jnp.repeat(jnp.exp(fresh - local_top[:, :, None]), RBLK, axis=2) * queries
    numerator = jnp.einsum(
        "bhkv,bhk->bhv", refreshed_cell, weight_matrix, precision=lax.Precision.HIGHEST
    )
    denom = jnp.sum(new_normal * weight_matrix, axis=2)
    top, numerator, denom = combined_all((local_top, numerator, denom), "row", combine_pairs)
    readout = numerator / jnp.maximum(jnp.abs(denom), jnp.exp(-top))[:, :, None]
    running_totals, squares = lax.psum(
        (jnp.sum(readout, axis=2), jnp.sum(readout * readout, axis=2)), "col"
    )
    mean = running_totals / DV
    var = squares / DV - mean * mean
    normed = (readout - mean[:, :, None]) * lax.rsqrt(var + 1e-06)[:, :, None]
    gated = (normed * norm_gain * jax.nn.sigmoid(output_gate_logits)).astype(jnp.bfloat16)
    seq_rows = gated.shape[0]
    out_cols = out_weight.shape[2]
    partial_value = jnp.dot(
        gated.reshape(seq_rows, -1),
        lax.all_gather(out_weight, "hb", axis=0, tiled=True).reshape(-1, out_cols),
        preferred_element_type=jnp.float32,
    )
    layer_out = lax.psum(partial_value, "col")
    return (layer_out, readout, refreshed_cell, new_normal, fresh)


def solution(mesh):
    placed = (
        P("hb", None, "row", "col"),
        P("hb", None, "row"),
        P("hb", None, "row"),
        P("hb", None, "row"),
        P("hb", None, "row"),
        P("hb", None, "col"),
        P("hb", None),
        P("hb", None),
        P("hb", None, "col"),
        P(None, "col"),
        P("hb", "col", "row"),
    )
    return jax.shard_map(
        local,
        mesh=mesh,
        in_specs=placed,
        out_specs=(
            P("hb", "row"),
            P("hb", None, "col"),
            P("hb", None, "row", "col"),
            P("hb", None, "row"),
            P("hb", None, "row"),
        ),
        check_vma=False,
    )
```

profile of v0, /device:TPU:0, one launch (start us, length us, event | category | flops | bytes accessed | tf_op | source)
XLA Modules:
  0.0 149.9 jit_solution(2049567945831490192)
XLA Ops:
  7.2 0.0 all-gather.7.cloned.1.call-start
  7.2 0.7 all-gather.7.cloned.1.call-update
  7.9 0.0 all-reduce.3.cloned.1.call-start
  7.9 0.7 fusion.3
  8.6 0.8 fusion.12
  9.5 0.0 copy-start.2
  9.5 0.8 subtract_exponential_fusion.1
  10.3 0.2 copy.55
  10.5 1.2 copy.61
  11.7 1.2 copy.58
  12.8 1.2 copy.56
  14.0 0.2 multiply_reduce_fusion
  14.2 5.3 %all-gather.3 = f32[2,64,8]{1,2,0:T(8,128)S(1)} all-gather(f32[1,64,8]{1,2,0:T(8,128)S(1)} %bitcast.66), channel_id=3, replica_groups=mesh['hb'=4,'row'=2,'col'=4] {'row'}, dimensions={0}, use_global_device_ids=true | all-gather | bytes 6144 | tf_op jit(solution)/shard_map/all_gather | solution.py:12
  19.5 4.3 %all-gather.4 = f32[2,64,8]{1,2,0:T(8,128)S(1)} all-gather(f32[1,64,8]{1,2,0:T(8,128)S(1)} %bitcast.67), channel_id=4, replica_groups=mesh['hb'=4,'row'=2,'col'=4] {'row'}, dimensions={0}, use_global_device_ids=true | all-gather | bytes 6144 | tf_op jit(solution)/shard_map/all_gather | solution.py:12
  23.9 0.1 copy.59
  24.0 0.1 copy.62
  24.1 0.1 copy.60
  24.1 0.2 copy.69
  24.4 0.2 copy.57
  24.6 23.3 %multiply_add_fusion = f32[64,8,128,128]{3,2,1,0:T(8,128)} fusion(f32[64,8,128,128]{3,2,1,0:T(8,128)} %param.11, f32[64,8,128]{2,1,0:T(8,128)} %param.16, f32[64,8,128]{2,1,0:T(8,128)S(1)} %copy.57, f32[64,8,128]{2,1,0:T(8,128)S(1)} %copy.55), kind=kLoop, calls=%fused_computation | loop fusion | flops 25165824 | bytes 67895296 | tf_op jit(solution)/shard_map/add | solution.py:50
  47.9 0.0 copy-done.2
  47.9 0.0 copy-start.1
  47.9 0.0 copy-start.3
  47.9 31.9 %fusion.13 = f32[64,8,1,128]{3,2,1,0:T(1,128)S(1)} fusion(f32[64,8,128,128]{3,2,1,0:T(8,128)} %multiply_add_fusion, f32[64,8,128,1]{2,3,1,0:T(1,128)S(1)} %copy.69), kind=kOutput, calls=%fused_computation.35 | convolution fusion | flops 100663296 | bytes 34078720 | tf_op jit(solution)/shard_map/bhkv,bhk->bhv/dot_general | solution.py:56
  79.9 7.0 %all-gather = f32[128,8,128]{2,1,0:T(8,128)S(1)} all-gather(f32[64,8,128]{2,1,0:T(8,128)S(1)} %bitcast.65), channel_id=2, replica_groups=mesh['hb'=4,'row'=2,'col'=4] {'row'}, dimensions={0}, use_global_device_ids=true | all-gather | bytes 786432 | tf_op jit(solution)/shard_map/all_gather | solution.py:12
  86.9 0.4 fusion.10
  87.3 0.0 copy-start
  87.4 0.1 copy.63
  87.4 0.1 copy.65
  87.5 12.7 %all-reduce = (f32[64,8]{0,1:T(8,128)S(1)}, f32[64,8]{0,1:T(8,128)S(1)}) all-reduce(f32[64,8]{0,1:T(8,128)S(1)} %copy.65, f32[64,8]{0,1:T(8,128)S(1)} %copy.63), channel_id=1, replica_groups=mesh['hb'=4,'row'=2,'col'=4] {'col'}, use_global_device_ids=true, to_apply=%region_5.6 | all-reduce | flops 1024 | bytes 8192 | tf_op jit(solution)/shard_map/psum | solution.py:62
  100.2 0.1 copy.64
  100.3 0.1 copy.66
  100.4 0.0 copy-done.1
  100.4 0.0 copy-done.3
  100.4 0.2 multiply_convert_fusion
  100.6 0.0 all-gather.7.cloned.1.call-done
  100.7 3.8 %convolution_bitcast_fusion = f32[64,2048]{1,0:T(8,128)} fusion(bf16[8,128,2048]{2,1,0:T(8,128)(2,1)} %all-gather.7.cloned.1.call-done, bf16[64,8,128]{2,1,0:T(8,128)(2,1)S(1)} %multiply_convert_fusion), kind=kOutput, calls=%fused_computation.1 | convolution fusion | flops 268435456 | bytes 4849664 | tf_op jit(solution)/shard_map/dot_general | solution.py:71
  104.5 0.0 all-reduce.3.cloned.1.call-update
  104.5 0.9 copy.68
  105.4 35.8 %all-reduce.3.cloned.1.call-done = f32[64,2048]{1,0:T(8,128)} async-done(((f32[64,2048]{1,0:T(8,128)}), f32[64,2048]{1,0:T(8,128)}) %all-reduce.3.cloned.1.call-update) | async-done | bytes 524304 | tf_op jit(solution)/shard_map/psum | solution.py:76
  141.2 1.9 %copy.74 = f32[64,2048]{1,0:T(8,128)} copy(f32[64,2048]{1,0:T(8,128)} %all-reduce.3.cloned.1.call-done) | data formatting | bytes 1048576
  143.1 0.0 copy-done
  (3 shorter events, 0.1 us)
Async XLA Ops:
  7.2 93.5 %all-gather.7.cloned.1.call-start = ((), (), s32[]{:S(2)}) async-start(), calls=%async_computation | async-start | bytes 5242880 | tf_op jit(solution)/shard_map/all_gather | solution.py:73
  7.9 133.3 %all-reduce.3.cloned.1.call-start = ((), (), s32[]{:S(2)}) async-start(), calls=%async_computation.1 | async-start | bytes 1048576 | tf_op jit(solution)/shard_map/psum | solution.py:76
  9.5 38.5 %copy-start.2 = (f32[64,8,8]{0,2,1:T(8,128)}, f32[64,8,8]{0,2,1:T(8,128)S(1)}, u32[]{:S(2)}) copy-start(f32[64,8,8]{0,2,1:T(8,128)S(1)} %get-tuple-element.72) | copy-start | bytes 49156
  47.9 52.5 %copy-start.1 = (f32[64,8,128]{2,1,0:T(8,128)S(1)}, f32[64,8,128]{2,1,0:T(8,128)}, u32[]{:S(2)}) copy-start(f32[64,8,128]{2,1,0:T(8,128)} %param.19) | copy-start | bytes 786436
  47.9 52.5 %copy-start.3 = (f32[8,128]{1,0:T(8,128)S(1)}, f32[8,128]{1,0:T(8,128)}, u32[]{:S(2)}) copy-start(f32[8,128]{1,0:T(8,128)} %param.20) | copy-start | bytes 12292
  87.3 55.7 %copy-start = (f32[64,8,128]{2,1,0:T(8,128)}, f32[64,8,128]{2,1,0:T(8,128)S(1)}, u32[]{:S(2)}) copy-start(f32[64,8,128]{2,1,0:T(8,128)S(1)} %get-tuple-element.69) | copy-start | bytes 786436
Sparse Core Ops, SparseCore 0:
  9.5 37.1 all-gather.6
  104.6 36.5 all-reduce.2
where the time goes:
time: 150 us
  waiting for transfers between devices  36.5 us (24%)
  matrix products  35.8 us (24%)
  blocking collectives  29.4 us (20%)
  other arithmetic  26.5 us (18%)
  between operations  14.2 us (9%)
  local copies, waits for them, and re-layouts  7.43 us (5%)
    psum x1, waiting for transfers between devices, local(): layer_out = lax.psum(partial_value, 'col')  35.8 us
    dot_general x1, matrix products, local(): jnp.einsum('bhkv,bhk->bhv', refreshed_cell, weight_matrix, precision=lax....  31.9 us
    add x1, other arithmetic, local(): keep[:, :, :, None] * cell_state  23.3 us
    all_gather x3, blocking collectives, combined_all(): gathered = jax.tree.map(lambda a: lax.all_gather(a, axis), part)  16.7 us
    psum x1, blocking collectives, local(): lax.psum((jnp.sum(readout, axis=2), jnp.sum(readout * readout, axis=2)),...  12.7 us
    unnamed x13, local copies, waits for them, and re-layouts  6.25 us
    dot_general x1, matrix products, local(): jnp.dot(gated.reshape(seq_rows, -1), lax.all_gather(out_weight, 'hb', axi...  3.83 us
  transfers between devices with their start and end apart: 2, of which 1 were waited for; matrix products, arithmetic and copies ran while one was open for 43% of the time, Pallas kernels for 0%

commit v1 on v0

--- a/solution.py
+++ b/solution.py
@@ -73,7 +73,13 @@
         lax.all_gather(out_weight, "hb", axis=0, tiled=True).reshape(-1, out_cols),
         preferred_element_type=jnp.float32,
     )
-    layer_out = lax.psum(partial_value, "col")
+    size = lax.axis_size("col")
+    layer_out, reach = (partial_value, 1)
+    while reach < size:
+        layer_out = layer_out + lax.ppermute(
+            layer_out, "col", [(i, i ^ reach) for i in range(size)]
+        )
+        reach = 2 * reach
     return (layer_out, readout, refreshed_cell, new_normal, fresh)
 
 

time: 150 us -> 140 us (0.933)
  waiting for transfers between devices: 36.5 us -> 27.8 us
  local copies, waits for them, and re-layouts: 7.43 us -> 5.55 us
    psum x1 -> x0, waiting for transfers between devices: 35.8 us -> none  [local(): layer_out = lax.psum(partial_value, 'col')]
    ppermute x0 -> x2, waiting for transfers between devices: none -> 27.1 us  [local(): lax.ppermute(layer_out, 'col', [(i, i ^ reach) for i in range(size)])]
    unnamed x13 -> x12, local copies, waits for them, and re-layouts: 6.25 us -> 4.38 us
  transfers between devices with their start and end apart: 2 -> 3, of which waited for: 1 -> 2; matrix products, arithmetic and copies ran while one was open for 43% -> 46% of each run, Pallas kernels for 0% -> 0%
where the time goes in v1:
time: 140 us
  matrix products  35 us (25%)
  blocking collectives  29.5 us (21%)
  waiting for transfers between devices  27.8 us (20%)
  other arithmetic  27.5 us (20%)
  between operations  14.2 us (10%)
  local copies, waits for them, and re-layouts  5.55 us (4%)
    dot_general x1, matrix products, local(): jnp.einsum('bhkv,bhk->bhv', refreshed_cell, weight_matrix, precision=lax....  31.9 us
    ppermute x2, waiting for transfers between devices, local(): lax.ppermute(layer_out, 'col', [(i, i ^ reach) for i in range(size)])  27.1 us
    add x1, other arithmetic, local(): keep[:, :, :, None] * cell_state  23.3 us
    all_gather x3, blocking collectives, combined_all(): gathered = jax.tree.map(lambda a: lax.all_gather(a, axis), part)  16.7 us
    psum x1, blocking collectives, local(): lax.psum((jnp.sum(readout, axis=2), jnp.sum(readout * readout, axis=2)),...  12.8 us
    unnamed x12, local copies, waits for them, and re-layouts  4.38 us
    dot_general x1, matrix products, local(): jnp.dot(gated.reshape(seq_rows, -1), lax.all_gather(out_weight, 'hb', axi...  3.03 us
  transfers between devices with their start and end apart: 3, of which 2 were waited for; matrix products, arithmetic and copies ran while one was open for 46% of the time, Pallas kernels for 0%

profile of v1, /device:TPU:0, one launch (start us, length us, event | category | flops | bytes accessed | tf_op | source)
XLA Modules:
  0.0 139.6 jit_solution(6251009202760472372)
XLA Ops:
  7.2 0.0 all-gather.7.cloned.1.call-start
  7.2 0.7 all-gather.7.cloned.1.call-update
  7.9 0.7 fusion.3
  8.6 0.8 fusion.12
  9.4 0.0 copy-start.2
  9.4 0.8 subtract_exponential_fusion.1
  10.3 0.2 copy.55
  10.5 1.2 copy.61
  11.6 1.2 copy.58
  12.8 1.2 copy.56
  14.0 0.2 multiply_reduce_fusion
  14.2 5.3 %all-gather.3 = f32[2,64,8]{1,2,0:T(8,128)S(1)} all-gather(f32[1,64,8]{1,2,0:T(8,128)S(1)} %bitcast.66), channel_id=3, replica_groups=mesh['hb'=4,'row'=2,'col'=4] {'row'}, dimensions={0}, use_global_device_ids=true | all-gather | bytes 6144 | tf_op jit(solution)/shard_map/all_gather | solution.py:12
  19.5 4.3 %all-gather.4 = f32[2,64,8]{1,2,0:T(8,128)S(1)} all-gather(f32[1,64,8]{1,2,0:T(8,128)S(1)} %bitcast.67), channel_id=4, replica_groups=mesh['hb'=4,'row'=2,'col'=4] {'row'}, dimensions={0}, use_global_device_ids=true | all-gather | bytes 6144 | tf_op jit(solution)/shard_map/all_gather | solution.py:12
  23.8 0.1 copy.59
  23.9 0.1 copy.62
  24.0 0.1 copy.60
  24.1 0.2 copy.69
  24.3 0.2 copy.57
  24.5 23.3 %multiply_add_fusion = f32[64,8,128,128]{3,2,1,0:T(8,128)} fusion(f32[64,8,128,128]{3,2,1,0:T(8,128)} %param.11, f32[64,8,128]{2,1,0:T(8,128)} %param.16, f32[64,8,128]{2,1,0:T(8,128)S(1)} %copy.57, f32[64,8,128]{2,1,0:T(8,128)S(1)} %copy.55), kind=kLoop, calls=%fused_computation | loop fusion | flops 25165824 | bytes 67895296 | tf_op jit(solution)/shard_map/add | solution.py:50
  47.8 0.0 copy-done.2
  47.9 0.0 copy-start.1
  47.9 0.0 copy-start.3
  47.9 31.9 %fusion.13 = f32[64,8,1,128]{3,2,1,0:T(1,128)S(1)} fusion(f32[64,8,128,128]{3,2,1,0:T(8,128)} %multiply_add_fusion, f32[64,8,128,1]{2,3,1,0:T(1,128)S(1)} %copy.69), kind=kOutput, calls=%fused_computation.35 | convolution fusion | flops 100663296 | bytes 34078720 | tf_op jit(solution)/shard_map/bhkv,bhk->bhv/dot_general | solution.py:56
  79.8 7.0 %all-gather = f32[128,8,128]{2,1,0:T(8,128)S(1)} all-gather(f32[64,8,128]{2,1,0:T(8,128)S(1)} %bitcast.65), channel_id=2, replica_groups=mesh['hb'=4,'row'=2,'col'=4] {'row'}, dimensions={0}, use_global_device_ids=true | all-gather | bytes 786432 | tf_op jit(solution)/shard_map/all_gather | solution.py:12
  86.9 0.4 fusion.10
  87.3 0.0 copy-start
  87.3 0.1 copy.63
  87.4 0.1 copy.65
  87.4 12.8 %all-reduce = (f32[64,8]{0,1:T(8,128)S(1)}, f32[64,8]{0,1:T(8,128)S(1)}) all-reduce(f32[64,8]{0,1:T(8,128)S(1)} %copy.65, f32[64,8]{0,1:T(8,128)S(1)} %copy.63), channel_id=1, replica_groups=mesh['hb'=4,'row'=2,'col'=4] {'col'}, use_global_device_ids=true, to_apply=%region_5.6 | all-reduce | flops 1024 | bytes 8192 | tf_op jit(solution)/shard_map/psum | solution.py:62
  100.3 0.1 copy.64
  100.3 0.1 copy.66
  100.4 0.0 copy-done.1
  100.4 0.0 copy-done.3
  100.4 0.2 multiply_convert_fusion
  100.6 0.0 all-gather.7.cloned.1.call-done
  100.7 3.0 %convolution_bitcast_fusion = f32[64,2048]{1,0:T(8,128)S(1)} fusion(bf16[8,128,2048]{2,1,0:T(8,128)(2,1)} %all-gather.7.cloned.1.call-done, bf16[64,8,128]{2,1,0:T(8,128)(2,1)S(1)} %multiply_convert_fusion), kind=kOutput, calls=%fused_computation.1 | convolution fusion | flops 268435456 | bytes 4849664 | tf_op jit(solution)/shard_map/dot_general | solution.py:71
  103.7 0.1 collective-permute-start
  103.8 11.7 %collective-permute-done = f32[64,2048]{1,0:T(8,128)S(1)} collective-permute-done((f32[64,2048]{1,0:T(8,128)S(1)}, f32[64,2048]{1,0:T(8,128)S(1)}, u32[]{:S(2)}, u32[]{:S(2)}) %collective-permute-start) | collective-permute-done | bytes 524320 | tf_op jit(solution)/shard_map/ppermute | solution.py:79
  115.5 0.1 add.73
  115.6 0.1 collective-permute-start.1
  115.7 0.9 copy.68
  116.5 15.4 %collective-permute-done.1 = f32[64,2048]{1,0:T(8,128)S(1)} collective-permute-done((f32[64,2048]{1,0:T(8,128)S(1)}, f32[64,2048]{1,0:T(8,128)S(1)}, u32[]{:S(2)}, u32[]{:S(2)}) %collective-permute-start.1) | collective-permute-done | bytes 524320 | tf_op jit(solution)/shard_map/ppermute | solution.py:79
  131.9 0.8 add.74
  132.8 0.0 copy-done
  (3 shorter events, 0.1 us)
Async XLA Ops:
  7.2 93.5 %all-gather.7.cloned.1.call-start = ((), (), s32[]{:S(2)}) async-start(), calls=%async_computation | async-start | bytes 5242880 | tf_op jit(solution)/shard_map/all_gather | solution.py:73
  9.4 38.4 %copy-start.2 = (f32[64,8,8]{0,2,1:T(8,128)}, f32[64,8,8]{0,2,1:T(8,128)S(1)}, u32[]{:S(2)}) copy-start(f32[64,8,8]{0,2,1:T(8,128)S(1)} %get-tuple-element.59) | copy-start | bytes 49156
  47.9 52.6 %copy-start.1 = (f32[64,8,128]{2,1,0:T(8,128)S(1)}, f32[64,8,128]{2,1,0:T(8,128)}, u32[]{:S(2)}) copy-start(f32[64,8,128]{2,1,0:T(8,128)} %param.19) | copy-start | bytes 786436
  47.9 52.6 %copy-start.3 = (f32[8,128]{1,0:T(8,128)S(1)}, f32[8,128]{1,0:T(8,128)}, u32[]{:S(2)}) copy-start(f32[8,128]{1,0:T(8,128)} %param.20) | copy-start | bytes 12292
  87.3 45.5 %copy-start = (f32[64,8,128]{2,1,0:T(8,128)}, f32[64,8,128]{2,1,0:T(8,128)S(1)}, u32[]{:S(2)}) copy-start(f32[64,8,128]{2,1,0:T(8,128)S(1)} %get-tuple-element.53) | copy-start | bytes 786436
  103.7 11.8 %collective-permute-start = (f32[64,2048]{1,0:T(8,128)S(1)}, f32[64,2048]{1,0:T(8,128)S(1)}, u32[]{:S(2)}, u32[]{:S(2)}) collective-permute-start(f32[64,2048]{1,0:T(8,128)S(1)} %convolution_bitcast_fusion), channel_id=1, source_target_pairs={{0,1},{1,0},{2,3},{3,2},{4,5},{5,4},{6,7},{7,6},{8,9},{9,8},{10,11... | collective-permute-start | bytes 1572872 | tf_op jit(solution)/shard_map/ppermute | solution.py:79
  115.6 16.4 %collective-permute-start.1 = (f32[64,2048]{1,0:T(8,128)S(1)}, f32[64,2048]{1,0:T(8,128)S(1)}, u32[]{:S(2)}, u32[]{:S(2)}) collective-permute-start(f32[64,2048]{1,0:T(8,128)S(1)} %add.73), channel_id=1, source_target_pairs={{0,2},{1,3},{2,0},{3,1},{4,6},{5,7},{6,4},{7,5},{8,10},{9,11},{10,... | collective-permute-start | bytes 1572872 | tf_op jit(solution)/shard_map/ppermute | solution.py:79
Sparse Core Ops, SparseCore 0:
  9.5 37.1 all-gather.6
